TPU v7x, 512 devices: a whole 4x4x16 slice. The times are simulated.
512 devices in a mesh: gz: 8 (over y, core), row: 16 (over z), col: 4 (over x).
Axes of the slice: x: 4, y: 4, z: 16, core: 2. Of those that a mesh axis runs over, the one named last changes fastest.
Arguments:
- lpanel: bfloat16 [2, 8, 4096, 2048], P(None, 'gz', 'row', 'col'), may hold values from -6 to 6
- upanel: bfloat16 [2, 8, 2048, 4096], P(None, 'gz', 'row', 'col'), may hold values from -0.125 to 0.125
- rowmap: int32 [2, 8, 16], P(None, 'gz', 'row'), may hold values from 0 to 1
- colmap: int32 [2, 8, 16], P(None, 'gz', 'col'), may hold values from 0 to 7
- blockmask: int32 [2, 8, 16, 16], P(None, 'gz', 'row', 'col'), may hold values 0 or 1
- front_blocks: bfloat16 [2, 8192, 8192], P(None, 'row', ('gz', 'col')), may hold values from -6 to 6
Outputs:
- front_update: bfloat16 [2, 8192, 8192], P(None, 'row', ('gz', 'col'))
All inputs are finite; a program needn't handle non-finite values. No bound on the sum of `blockmask` on one device may be relied on, other than what follows from the above.
Results may differ from a plain program's by a relative error of at most 0.008.
Values may be sent and summed in bfloat16 or wider, within the bound.
A program may use at most 64 MiB of HBM per device.

v0:
```python
import jax
import jax.numpy as jnp
from jax import lax
from jax.sharding import PartitionSpec as P

CB = 4
FRB = 2
LEVELS = 2


def copy_for_each(value, axis):
    copies = jnp.broadcast_to(value, (lax.axis_size(axis), *value.shape))
    return lax.all_to_all(copies, axis, split_axis=0, concat_axis=0, tiled=True)


def in_order(pieces, dim):
    pieces = jnp.moveaxis(pieces, 0, dim)
    shape = pieces.shape
    return pieces.reshape(*shape[:dim], shape[dim] * shape[dim + 1], *shape[dim + 2 :])


def gathered_copies(value, axis, dim):
    pieces = copy_for_each(value, axis)
    return in_order(pieces, dim)


def column_sums(schur, cols_of, live, layers):
    width = schur.shape[0]
    blocks = schur.reshape(width, CB, width)
    targets = cols_of[:, None] == jnp.arange(layers, dtype=jnp.int32)[None, :]
    col_select = targets.astype(jnp.float32) * live.astype(jnp.float32)[:, None]
    return jnp.einsum("bjk,jl->lbk", blocks, col_select)


def on_device(lpanel, upanel, rowmap, colmap, blockmask, front_blocks):
    layers = lax.axis_size("gz")
    width = lpanel.shape[2]
    tiles = []
    left_all = gathered_copies(lpanel[:, 0], "col", 2)
    schur_all = jnp.einsum(
        "vbk,vkn->vbn",
        left_all,
        lax.all_gather(upanel[:, 0], "row", axis=1, tiled=True),
        preferred_element_type=jnp.float32,
    )
    for depth in range(LEVELS):
        tiles.append(schur_all[depth])
    results = []
    every_row = gathered_copies(rowmap[:, :, 0], "gz", 1)
    for depth in range(LEVELS):
        sums = column_sums(tiles[depth], colmap[depth, 0], blockmask[depth, 0, 0], layers).astype(
            jnp.bfloat16
        )
        arrived = lax.all_to_all(sums, "gz", split_axis=0, concat_axis=0, tiled=True)
        row_select = (
            every_row[depth][:, None] == jnp.arange(FRB, dtype=jnp.int32)[None, :]
        ).astype(jnp.float32)
        placed = jnp.einsum("sf,sbk->fbk", row_select, arrived.astype(jnp.float32))
        placed = placed.reshape(FRB * width, width)
        results.append((front_blocks[depth].astype(jnp.float32) - placed).astype(jnp.bfloat16))
    return jnp.stack(results)


def solution(mesh):
    return jax.shard_map(
        on_device,
        mesh=mesh,
        in_specs=(
            P(None, "gz", "row", "col"),
            P(None, "gz", "row", "col"),
            P(None, "gz", "row"),
            P(None, "gz", "col"),
            P(None, "gz", "row", "col"),
            P(None, "row", ("gz", "col")),
        ),
        out_specs=P(None, "row", ("gz", "col")),
        check_vma=False,
    )
```

profile of v0, /device:TPU:1, one launch (start us, length us, event | category | flops | bytes accessed | tf_op | source)
XLA Modules:
  0.0 177.1 jit_solution(10391347468096292593)
XLA Ops:
  6.5 0.0 all-gather.3.cloned.1.call-start
  6.5 0.7 all-gather.3.cloned.1.call-update
  7.3 2.6 %broadcast_in_dim.5 = bf16[4,2,256,512]{3,2,1,0:T(8,128)(2,1)} broadcast(bf16[2,256,512]{2,1,0:T(8,128)(2,1)} %bitcast.46), dimensions={1,2,3} | broadcast | bytes 2621440 | tf_op jit(solution)/shard_map/broadcast_in_dim | solution.py:12
  9.8 0.0 copy-start.1
  9.9 0.0 copy-start.2
  9.9 0.0 copy-start.3
  9.9 5.0 %all-to-all-start.1 = ((bf16[4,2,256,512]{3,2,1,0:T(8,128)(2,1)}), bf16[4,2,256,512]{3,2,1,0:T(8,128)(2,1)S(1)}, u32[]{:S(2)}, u32[]{:S(2)}) async-start(bf16[4,2,256,512]{3,2,1,0:T(8,128)(2,1)} %broadcast_in_dim.5), calls=%async_computation.1 | async-start | bytes 4194304 | tf_op jit(solution)/shard_map/all_to_all | solution.py:13
  14.8 0.0 copy-done.1
  14.8 0.0 copy-done.2
  14.8 20.5 %all-to-all-done.1 = bf16[4,2,256,512]{3,2,1,0:T(8,128)(2,1)S(1)} async-done(((bf16[4,2,256,512]{3,2,1,0:T(8,128)(2,1)}), bf16[4,2,256,512]{3,2,1,0:T(8,128)(2,1)S(1)}, u32[]{:S(2)}, u32[]{:S(2)}) %all-to-all-start.1) | async-done | bytes 2097184 | tf_op jit(solution)/shard_map/all_to_all | solution.py:13
  35.4 0.0 copy-done.3
  35.4 0.6 broadcast_in_dim.4
  36.0 11.2 %all-to-all-start = ((s32[8,2,1]{1,2,0:T(1,128)}), s32[8,2,1]{1,2,0:T(1,128)S(1)}, u32[]{:S(2)}, u32[]{:S(2)}) async-start(s32[8,2,1]{1,2,0:T(1,128)} %broadcast_in_dim.4), calls=%async_computation | async-start | bytes 8192 | tf_op jit(solution)/shard_map/all_to_all | solution.py:13
  47.2 1.6 copy.35
  48.8 71.7 %all-gather.3.cloned.1.call-done = bf16[2,1,2048,1024]{3,2,0,1:T(8,128)(2,1)} async-done(((bf16[2,1,128,1024]{3,2,0,1:T(8,128)(2,1)}), bf16[2,1,2048,1024]{3,2,0,1:T(8,128)(2,1)}) %all-gather.3.cloned.1.call-update) | async-done | bytes 8388624 | tf_op jit(solution)/shard_map/all_gather | solution.py:43
  120.5 6.3 %fusion = bf16[2,256,1024]{2,1,0:T(8,128)(2,1)S(1)} fusion(bf16[2,256,2048]{2,1,0:T(8,128)(2,1)} %bitcast.43, bf16[2,1,2048,1024]{3,2,0,1:T(8,128)(2,1)} %all-gather.3.cloned.1.call-done), kind=kOutput, calls=%fused_computation | convolution fusion | flops 2147483648 | bytes 11534336 | tf_op jit(solution)/shard_map/vbk,vkn->vbn/dot_general | solution.py:40
  126.8 0.1 fusion.28
  126.9 0.4 reshape_squeeze.7
  127.3 0.6 convolution_convert_fusion
  127.8 1.2 copy.32
  129.0 0.0 all-to-all-done
  129.0 5.1 %all-to-all-start.3 = ((bf16[8,256,256]{2,1,0:T(8,128)(2,1)}), bf16[8,256,256]{2,1,0:T(8,128)(2,1)S(1)}, u32[]{:S(2)}, u32[]{:S(2)}) async-start(bf16[8,256,256]{2,1,0:T(8,128)(2,1)} %copy.32), calls=%async_computation.3 | async-start | bytes 2097152 | tf_op jit(solution)/shard_map/all_to_all | solution.py:54
  134.2 0.4 reshape_squeeze.6
  134.5 0.6 convolution_convert_fusion.1
  135.1 1.2 copy.29
  136.3 12.8 %all-to-all-done.3 = bf16[8,256,256]{2,1,0:T(8,128)(2,1)S(1)} async-done(((bf16[8,256,256]{2,1,0:T(8,128)(2,1)}), bf16[8,256,256]{2,1,0:T(8,128)(2,1)S(1)}, u32[]{:S(2)}, u32[]{:S(2)}) %all-to-all-start.3) | async-done | bytes 1048608 | tf_op jit(solution)/shard_map/all_to_all | solution.py:54
  149.1 4.4 %all-to-all-start.2 = ((bf16[8,256,256]{2,1,0:T(8,128)(2,1)}), bf16[8,256,256]{2,1,0:T(8,128)(2,1)S(1)}, u32[]{:S(2)}, u32[]{:S(2)}) async-start(bf16[8,256,256]{2,1,0:T(8,128)(2,1)} %copy.29), calls=%async_computation.2 | async-start | bytes 2097152 | tf_op jit(solution)/shard_map/all_to_all | solution.py:54
  153.6 0.4 slice_reduce_fusion.1
  153.9 0.7 fusion.2
  154.7 0.0 copy-start
  154.7 13.8 %all-to-all-done.2 = bf16[8,256,256]{2,1,0:T(8,128)(2,1)S(1)} async-done(((bf16[8,256,256]{2,1,0:T(8,128)(2,1)}), bf16[8,256,256]{2,1,0:T(8,128)(2,1)S(1)}, u32[]{:S(2)}, u32[]{:S(2)}) %all-to-all-start.2) | async-done | bytes 1048608 | tf_op jit(solution)/shard_map/all_to_all | solution.py:54
  168.6 0.7 fusion.4
  169.3 0.0 copy-done
  169.3 0.1 fusion.7
  169.5 0.0 copy-start.4
  169.5 0.8 copy-done.4
  (5 shorter events, 0.1 us)
Async XLA Ops:
  6.5 113.9 %all-gather.3.cloned.1.call-start = ((), (), s32[]{:S(2)}) async-start(), calls=%async_computation.4 | async-start | bytes 8912896 | tf_op jit(solution)/shard_map/all_gather | solution.py:43
  9.8 5.0 %copy-start.1 = (s32[2,1,4]{2,1,0:T(1,128)S(1)}, s32[2,1,4]{2,1,0:T(1,128)}, u32[]{:S(2)}) copy-start(s32[2,1,4]{2,1,0:T(1,128)} %param.9) | copy-start | bytes 100
  9.9 5.0 %copy-start.2 = (s32[2,1,1,4]{3,2,1,0:T(1,128)S(1)}, s32[2,1,1,4]{3,2,1,0:T(1,128)}, u32[]{:S(2)}) copy-start(s32[2,1,1,4]{3,2,1,0:T(1,128)} %param.10) | copy-start | bytes 100
  9.9 25.5 %copy-start.3 = (s32[2,1,1]{0,2,1:T(1,128)S(1)}, s32[2,1,1]{0,2,1:T(1,128)}, u32[]{:S(2)}) copy-start(s32[2,1,1]{0,2,1:T(1,128)} %param.8) | copy-start | bytes 28
  9.9 25.5 %all-to-all-start.1 = ((bf16[4,2,256,512]{3,2,1,0:T(8,128)(2,1)}), bf16[4,2,256,512]{3,2,1,0:T(8,128)(2,1)S(1)}, u32[]{:S(2)}, u32[]{:S(2)}) async-start(bf16[4,2,256,512]{3,2,1,0:T(8,128)(2,1)} %broadcast_in_dim.5), calls=%async_computation.1 | async-start | bytes 4194304 | tf_op jit(solution)/shard_map/all_to_all | solution.py:13
  36.0 93.1 %all-to-all-start = ((s32[8,2,1]{1,2,0:T(1,128)}), s32[8,2,1]{1,2,0:T(1,128)S(1)}, u32[]{:S(2)}, u32[]{:S(2)}) async-start(s32[8,2,1]{1,2,0:T(1,128)} %broadcast_in_dim.4), calls=%async_computation | async-start | bytes 8192 | tf_op jit(solution)/shard_map/all_to_all | solution.py:13
  129.0 20.1 %all-to-all-start.3 = ((bf16[8,256,256]{2,1,0:T(8,128)(2,1)}), bf16[8,256,256]{2,1,0:T(8,128)(2,1)S(1)}, u32[]{:S(2)}, u32[]{:S(2)}) async-start(bf16[8,256,256]{2,1,0:T(8,128)(2,1)} %copy.32), calls=%async_computation.3 | async-start | bytes 2097152 | tf_op jit(solution)/shard_map/all_to_all | solution.py:54
  149.1 19.4 %all-to-all-start.2 = ((bf16[8,256,256]{2,1,0:T(8,128)(2,1)}), bf16[8,256,256]{2,1,0:T(8,128)(2,1)S(1)}, u32[]{:S(2)}, u32[]{:S(2)}) async-start(bf16[8,256,256]{2,1,0:T(8,128)(2,1)} %copy.29), calls=%async_computation.2 | async-start | bytes 2097152 | tf_op jit(solution)/shard_map/all_to_all | solution.py:54
  154.7 14.6 %copy-start = (bf16[2,512,256]{2,1,0:T(8,128)(2,1)S(1)}, bf16[2,512,256]{2,1,0:T(8,128)(2,1)}, u32[]{:S(2)}) copy-start(bf16[2,512,256]{2,1,0:T(8,128)(2,1)} %param.11) | copy-start | bytes 1572868
  169.5 0.8 copy-start.4
Sparse Core Ops, SparseCore 0:
  9.4 110.9 all-gather.2
where the time goes:
time: 177 us
  waiting for transfers between devices  120 us (68%)
  starting transfers between devices  25.7 us (15%)
  between operations  13.5 us (8%)
  local copies, waits for them, and re-layouts  9.29 us (5%)
  matrix products  8.94 us (5%)
    all_gather x1, waiting for transfers between devices, on_device(): lax.all_gather(upanel[:, 0], 'row', axis=1, tiled=True)  71.7 us
    all_to_all x2, waiting for transfers between devices, on_device(): lax.all_to_all(sums, 'gz', split_axis=0, concat_axis=0, tiled=True)  26.7 us
    all_to_all x2, waiting for transfers between devices, copy_for_each(): return lax.all_to_all(copies, axis, split_axis=0, concat_axis=0, tiled=True)  20.5 us
    all_to_all x2, starting transfers between devices, copy_for_each(): return lax.all_to_all(copies, axis, split_axis=0, concat_axis=0, tiled=True)  16.2 us
    all_to_all x2, starting transfers between devices, on_device(): lax.all_to_all(sums, 'gz', split_axis=0, concat_axis=0, tiled=True)  9.55 us
    dot_general x1, matrix products, on_device(): jnp.einsum('vbk,vkn->vbn', left_all, lax.all_gather(upanel[:, 0], 'row',...  6.35 us
  transfers between devices with their start and end apart: 5, of which 4 were waited for; matrix products, arithmetic and copies ran while one was open for 9% of the time, Pallas kernels for 0%

commit v1 on v0

v1 whole, which is shorter than its diff:
```python
import functools

import jax
import jax.numpy as jnp
from jax import lax
from jax.experimental import pallas as pl
from jax.experimental.pallas import tpu as pltpu
from jax.sharding import PartitionSpec as P

MESH = pl.DeviceIdType.MESH
CB = 4
FRB = 2
LEVELS = 2
HALVES = 2
SUBS = 4


def kernel(
    n_row, n_gz, n_col,
    l_hbm, u_hbm, rowmap_hbm, colmap_hbm, mask_hbm, front_hbm,
    out_hbm,
    u_all, l_all, acc, sums, arrived, rows_of, front, result,
    rowmap, colmap, mask,
    zsend, zrecv, lsend, lrecv, asend, arecv, rsend, rrecv, usem, lsem, fsem, osem, isem,
):
    row, gz, col = lax.axis_index("row"), lax.axis_index("gz"), lax.axis_index("col")
    phases = LEVELS * HALVES
    depth = u_hbm.shape[2]
    width = l_hbm.shape[2]
    half = width // HALVES
    lblocks = l_hbm.shape[3] // depth
    last = n_row // 2 - 1
    piece = depth // SUBS
    ring = [lax.rem(row + 1, n_row), lax.rem(row + n_row - 1, n_row)]

    def others(me, n):
        return [lax.rem(me + i, n) for i in range(1, n)]

    cores = 2
    chips = n_gz // cores
    chip, core = lax.div(gz, cores), lax.rem(gz, cores)
    order = sorted(range(1, chips), key=lambda d: -min(d, chips - d)) + [0]
    peers = []
    for d in order:
        for k in range(cores):
            if (d, k) != (0, 0):
                peers.append(lax.rem(chip + d, chips) * cores + lax.rem(core + k, cores))

    def own_u(p, j):
        v, h = divmod(p, HALVES)
        return pltpu.make_async_copy(
            u_hbm.at[v, 0, :, pl.ds(j * width + h * half, half)],
            u_all.at[p, pl.ds(row * depth, depth), pl.ds(j * half, half)],
            usem.at[p, j],
        )

    def own_l(v, i):
        return pltpu.make_async_copy(
            l_hbm.at[v, 0, :, pl.ds(i * depth, depth)], l_all.at[v, col * lblocks + i], lsem.at[v, i]
        )

    fronts = pltpu.make_async_copy(front_hbm, front, fsem)
    maps = [
        pltpu.make_async_copy(rowmap_hbm, rowmap, isem.at[0]),
        pltpu.make_async_copy(colmap_hbm, colmap, isem.at[1]),
        pltpu.make_async_copy(mask_hbm, mask, isem.at[2]),
    ]
    for j in range(CB):
        own_u(0, j).start()
    for i in range(lblocks):
        own_l(0, i).start()
    for p in range(1, phases):
        for j in range(CB):
            own_u(p, j).start()
    for v in range(1, LEVELS):
        for i in range(lblocks):
            own_l(v, i).start()
    fronts.start()
    for copy in maps:
        copy.start()

    barrier = pltpu.get_barrier_semaphore()
    for r in ring:
        pl.semaphore_signal(barrier, inc=1, device_id={"row": r}, device_id_type=MESH)
    for c in others(col, n_col):
        pl.semaphore_signal(barrier, inc=1, device_id={"col": c}, device_id_type=MESH)
    for g in peers:
        pl.semaphore_signal(barrier, inc=1, device_id={"gz": g}, device_id_type=MESH)
    pl.semaphore_wait(barrier, 2 + (n_col - 1) + (n_gz - 1))

    def hop(way, p, t, s):
        shard = lax.rem(row + n_row - t, n_row) if way == 0 else lax.rem(row + t, n_row)
        at = u_all.at[p, pl.ds(pl.multiple_of(shard * depth + s * piece, piece), piece)]
        return pltpu.make_async_remote_copy(
            src_ref=at, dst_ref=at, send_sem=zsend.at[way, p], recv_sem=zrecv.at[way, p, t, s],
            device_id={"row": ring[way]}, device_id_type=MESH,
        )

    def arrival(way, p, t, s):
        at = u_all.at[p, pl.ds(0, piece)]
        return pltpu.make_async_copy(at, at, zrecv.at[way, p, t, s])

    longer = (range(SUBS // 2), range(SUBS // 2, SUBS))

    def send_own(p):
        for j in range(CB):
            own_u(p, j).wait()
        for s in range(SUBS):
            for way in range(2):
                hop(way, p, 0, (s + way * SUBS // 2) % SUBS).start()

    def forward(p, t):
        for s in range(SUBS):
            for way in range(2):
                which = (s + way * SUBS // 2) % SUBS
                arrival(way, p, t - 1, which).wait()
                hop(way, p, t, which).start()

    def forward_last(p):
        for s in range(SUBS):
            for way in range(2):
                which = (s + way * SUBS // 2) % SUBS
                arrival(way, p, last - 1, which).wait()
                if which in longer[way]:
                    hop(way, p, last, which).start()

    def wait_last(p):
        for way in range(2):
            for s in longer[way]:
                arrival(way, p, last, s).wait()

    def l_copy(v, c):
        at = l_all.at[v, pl.ds(col * lblocks, lblocks)]
        return pltpu.make_async_remote_copy(
            src_ref=at, dst_ref=at, send_sem=lsend, recv_sem=lrecv.at[v, col],
            device_id={"col": c}, device_id_type=MESH,
        )

    def send_l(v):
        for i in range(lblocks):
            own_l(v, i).wait()
        for c in others(col, n_col):
            l_copy(v, c).start()

    def wait_l(v):
        at = l_all.at[v, pl.ds(0, lblocks)]
        for c in others(col, n_col):
            pltpu.make_async_copy(at, at, lrecv.at[v, c]).wait()

    def rows_copy(g):
        at = rows_of.at[gz]
        return pltpu.make_async_remote_copy(
            src_ref=at, dst_ref=at, send_sem=rsend, recv_sem=rrecv.at[gz],
            device_id={"gz": g}, device_id_type=MESH,
        )

    def wait_rows():
        at = rows_of.at[0]
        for g in peers:
            pltpu.make_async_copy(at, at, rrecv.at[g]).wait()

    def product(p, first, count):
        v = p // HALVES
        left = jnp.concatenate([l_all[v, first + i] for i in range(count)], axis=1) if count > 1 else l_all[v, first]
        right = u_all[p, pl.ds(pl.multiple_of(first * depth, depth), count * depth), :]
        return jnp.dot(left, right, preferred_element_type=jnp.float32)

    def products(p, q, parts):
        size = n_row // parts
        value = product(p, q * size, size)
        if q == 0:
            acc[p % 2] = value
        else:
            acc[p % 2] += value

    def block_copy(p, g):
        return pltpu.make_async_remote_copy(
            src_ref=sums.at[p, g], dst_ref=arrived.at[p, gz], send_sem=asend.at[p], recv_sem=arecv.at[p, gz],
            device_id={"gz": g}, device_id_type=MESH,
        )

    def layer_sum(p, g):
        v = p // HALVES
        total = None
        for j in range(CB):
            keep = jnp.where(colmap[v, 0, j] == g, mask[v, 0, 0, j], 0).astype(jnp.float32)
            term = acc[p % 2, :, j * half : (j + 1) * half] * keep
            total = term if total is None else total + term
        return total.astype(jnp.bfloat16)

    def exchange(p):
        before = None
        for g in peers:
            sums[p, g] = layer_sum(p, g)
            if before is not None:
                block_copy(p, before).start()
            before = g
        arrived[p, gz] = layer_sum(p, gz)
        block_copy(p, before).start()

    def out_copy(p):
        v, h = divmod(p, HALVES)
        at = (v, slice(None), pl.ds(h * half, half))
        return pltpu.make_async_copy(result.at[at], out_hbm.at[at], osem.at[p])

    def finish(p):
        v, h = divmod(p, HALVES)
        block = arrived.at[p, 0]
        for g in peers:
            pltpu.make_async_copy(block, block, arecv.at[p, g]).wait()
        placed = [None] * FRB
        for g in range(n_gz):
            value = arrived[p, g].astype(jnp.float32)
            target = rows_of[g, v][:1]
            for f in range(FRB):
                term = jnp.where(target == f, 1.0, 0.0).astype(jnp.float32) * value
                placed[f] = term if placed[f] is None else placed[f] + term
        for f in range(FRB):
            at = (v, slice(f * width, (f + 1) * width), slice(h * half, (h + 1) * half))
            result[at] = (front[at].astype(jnp.float32) - placed[f]).astype(jnp.bfloat16)
        out_copy(p).start()

    parts = 4
    send_own(0)
    send_l(0)
    for copy in maps:
        copy.wait()
    for v in range(LEVELS):
        rows_of[gz, v] = jnp.full(rows_of.shape[2:], rowmap[0, 0, v], jnp.int32)
    for p in range(phases):
        if p == 0:
            def body(t, _):
                forward(0, t)
                return 0
            lax.fori_loop(1, 3, body, 0)
            for v in range(1, LEVELS):
                send_l(v)
            for g in peers:
                rows_copy(g).start()
            lax.fori_loop(3, last, body, 0)
        elif p < phases - 1:
            for t in range(1, last):
                forward(p, t)
                if t == 1:
                    wait_last(p - 1)
                    if p == 1:
                        wait_l(0)
                if t <= parts:
                    products(p - 1, t - 1, parts)
                if t == parts:
                    exchange(p - 1)
                if t == 3 and p >= 2:
                    finish(p - 2)
        else:
            for t in range(1, last):
                forward(p, t)
                if t == 1:
                    wait_last(p - 1)
                if t <= 2:
                    products(p - 1, 2 * t - 2, parts)
                    products(p - 1, 2 * t - 1, parts)
                if t == 2:
                    exchange(p - 1)
                    acc[p % 2] = product(p, row, 1)
                if t == 3:
                    finish(p - 2)
                if t >= 3:
                    for d in ((1, 2, 3) if t == 3 else (t,)):
                        acc[p % 2] += product(p, lax.rem(row + d, n_row), 1)
                        acc[p % 2] += product(p, lax.rem(row + n_row - d, n_row), 1)
        if p < phases - 1:
            send_own(p + 1)
        if p == 0:
            fronts.wait()
            wait_rows()
        forward_last(p)
        if p == 1:
            wait_l(1)
    p = phases - 1
    finish(p - 1)
    acc[p % 2] += product(p, lax.rem(row + last, n_row), 1)
    acc[p % 2] += product(p, lax.rem(row + n_row - last, n_row), 1)
    wait_last(p)
    acc[p % 2] += product(p, lax.rem(row + last + 1, n_row), 1)
    exchange(p)
    finish(p)

    for way in range(2):
        for q in range(phases):
            at = u_all.at[q, pl.ds(0, depth * last + depth // 2)]
            pltpu.make_async_copy(at, at, zsend.at[way, q]).wait()
    at = l_all.at[pl.ds(0, LEVELS), pl.ds(0, (n_col - 1) * lblocks)]
    pltpu.make_async_copy(at, at, lsend).wait()
    at = rows_of.at[pl.ds(0, n_gz - 1)]
    pltpu.make_async_copy(at, at, rsend).wait()
    for q in range(phases):
        at = sums.at[q, pl.ds(0, n_gz - 1)]
        pltpu.make_async_copy(at, at, asend.at[q]).wait()
    for q in range(phases):
        out_copy(q).wait()


def on_device(lpanel, upanel, rowmap, colmap, blockmask, front_blocks):
    n_row, n_gz, n_col = lax.axis_size("row"), lax.axis_size("gz"), lax.axis_size("col")
    depth = upanel.shape[2]
    width = lpanel.shape[2]
    half = width // HALVES
    phases = LEVELS * HALVES
    lblocks = lpanel.shape[3] // depth
    hops = n_row // 2
    anywhere = pl.BlockSpec(memory_space=pltpu.HBM)
    dma = pltpu.SemaphoreType.DMA
    return pl.pallas_call(
        functools.partial(kernel, n_row, n_gz, n_col),
        out_shape=jax.ShapeDtypeStruct(front_blocks.shape, jnp.bfloat16),
        in_specs=[anywhere] * 6,
        out_specs=anywhere,
        scratch_shapes=[
            pltpu.VMEM((phases, n_row * depth, CB * half), jnp.bfloat16),
            pltpu.VMEM((LEVELS, n_row, width, depth), jnp.bfloat16),
            pltpu.VMEM((2, width, CB * half), jnp.float32),
            pltpu.VMEM((phases, n_gz, width, half), jnp.bfloat16),
            pltpu.VMEM((phases, n_gz, width, half), jnp.bfloat16),
            pltpu.VMEM((n_gz, LEVELS, 8, 128), jnp.int32),
            pltpu.VMEM(front_blocks.shape, jnp.bfloat16),
            pltpu.VMEM(front_blocks.shape, jnp.bfloat16),
            pltpu.SMEM((1, 1, LEVELS), jnp.int32),
            pltpu.SMEM(colmap.shape, jnp.int32),
            pltpu.SMEM(blockmask.shape, jnp.int32),
            dma((2, phases)),
            dma((2, phases, hops, SUBS)),
            dma,
            dma((LEVELS, n_col)),
            dma((phases,)),
            dma((phases, n_gz)),
            dma,
            dma((n_gz,)),
            dma((phases, CB)),
            dma((LEVELS, lblocks)),
            dma,
            dma((phases,)),
            dma((3,)),
        ],
        compiler_params=pltpu.CompilerParams(
            collective_id=0, has_side_effects=True, vmem_limit_bytes=67043328
        ),
    )(lpanel, upanel, jnp.transpose(rowmap, (1, 2, 0)), colmap, blockmask, front_blocks)


def solution(mesh):
    return jax.shard_map(
        on_device,
        mesh=mesh,
        in_specs=(
            P(None, "gz", "row", "col"),
            P(None, "gz", "row", "col"),
            P(None, "gz", "row"),
            P(None, "gz", "col"),
            P(None, "gz", "row", "col"),
            P(None, "row", ("gz", "col")),
        ),
        out_specs=P(None, "row", ("gz", "col")),
        check_vma=False,
    )
```

time: 177 us -> 125 us (0.71)
  Pallas kernels: 0 us -> 123 us
  waiting for transfers between devices: 120 us -> 0 us
  starting transfers between devices: 25.7 us -> 0 us
  between operations: 13.5 us -> 0.01 us
  matrix products: 8.94 us -> 0 us
  local copies, waits for them, and re-layouts: 9.29 us -> 1.87 us
    pallas_call x0 -> x1, Pallas kernels: none -> 123 us  [on_device(): pl.pallas_call(functools.partial(kernel, n_row, n_gz, n_col), out_shape=j...]
    all_gather x1 -> x0, waiting for transfers between devices: 71.7 us -> none  [on_device(): lax.all_gather(upanel[:, 0], 'row', axis=1, tiled=True)]
    all_to_all x4 -> x0, waiting for transfers between devices: 47.2 us -> none  [the longest x2 26.7 us: on_device(): lax.all_to_all(sums, 'gz', split_axis=0, concat_axis=0, tiled=True)]
    all_to_all x4 -> x0, starting transfers between devices: 25.7 us -> none  [the longest x2 16.2 us: copy_for_each(): return lax.all_to_all(copies, axis, split_axis=0, concat_axis=0, tiled=True)]
    dot_general x5 -> x0, matrix products: 8.94 us -> none  [the longest x1 6.35 us: on_device(): jnp.einsum('vbk,vkn->vbn', left_all, lax.all_gather(upanel[:, 0], 'row',...]
    broadcast_in_dim x2 -> x0, local copies, waits for them, and re-layouts: 3.19 us -> none  [copy_for_each(): copies = jnp.broadcast_to(value, (lax.axis_size(axis), *value.shape))]
    convert_element_type x2 -> x0, local copies, waits for them, and re-layouts: 2.38 us -> none  [on_device(): column_sums(tiles[depth], colmap[depth, 0], blockmask[depth, 0, 0], layers)]
  transfers between devices with their start and end apart: 5 -> 0, of which waited for: 4 -> 0; matrix products, arithmetic and copies ran while one was open for 9% -> 0% of each run, Pallas kernels for 0% -> 0%
where the time goes in v1:
time: 125 us
  Pallas kernels  123 us (98%)
  local copies, waits for them, and re-layouts  1.87 us (1%)
    pallas_call x1, Pallas kernels, on_device(): pl.pallas_call(functools.partial(kernel, n_row, n_gz, n_col), out_shape=j...  123 us

profile of v1, /device:TPU:1, one launch (start us, length us, event | category | flops | bytes accessed | tf_op | source)
XLA Modules:
  0.0 124.8 jit_solution(8808364113674946829)
XLA Ops:
  0.0 122.9 %shard_map.64 = bf16[2,512,256]{2,1,0:T(8,128)(2,1)} custom-call(bf16[2,1,256,512]{3,2,1,0:T(8,128)(2,1)} %l_hbm.1, bf16[2,1,128,1024]{3,2,1,0:T(8,128)(2,1)} %u_hbm.1, s32[1,1,2]{2,1,0:T(1,128)} %bitcast.1, s32[2,1,4]{2,1,0:T(1,128)} %colmap_hbm.1, s32[2,1,1,4]{3,2,1,0:T(1,128)} %mask_hbm.1, bf16[2,512,256]{2,1,0:T(8,128)(2,1)} %front_hbm.1), custom_call_target="tpu_custom_call" | custom-call | tf_op jit(solution)/shard_map/pallas_call | solution.py:313
  122.9 1.9 %copy.8 = bf16[2,512,256]{2,1,0:T(8,128)(2,1)} copy(bf16[2,512,256]{2,1,0:T(8,128)(2,1)} %shard_map.64) | data formatting | bytes 1048576

commit v2 on v1

--- a/solution.py
+++ b/solution.py
@@ -18,10 +18,10 @@
 def kernel(
     n_row, n_gz, n_col,
     l_hbm, u_hbm, rowmap_hbm, colmap_hbm, mask_hbm, front_hbm,
-    out_hbm,
-    u_all, l_all, acc, sums, arrived, rows_of, front, result,
+    out_ref,
+    u_all, l_all, acc, sums, arrived, rows_of, front,
     rowmap, colmap, mask,
-    zsend, zrecv, lsend, lrecv, asend, arecv, rsend, rrecv, usem, lsem, fsem, osem, isem,
+    zsend, zrecv, lsend, lrecv, asend, arecv, rsend, rrecv, usem, lsem, fsem, isem,
 ):
     row, gz, col = lax.axis_index("row"), lax.axis_index("gz"), lax.axis_index("col")
     phases = LEVELS * HALVES
@@ -169,9 +169,9 @@
         size = n_row // parts
         value = product(p, q * size, size)
         if q == 0:
-            acc[p % 2] = value
+            acc[p] = value
         else:
-            acc[p % 2] += value
+            acc[p] += value
 
     def block_copy(p, g):
         return pltpu.make_async_remote_copy(
@@ -184,7 +184,7 @@
         total = None
         for j in range(CB):
             keep = jnp.where(colmap[v, 0, j] == g, mask[v, 0, 0, j], 0).astype(jnp.float32)
-            term = acc[p % 2, :, j * half : (j + 1) * half] * keep
+            term = acc[p, :, j * half : (j + 1) * half] * keep
             total = term if total is None else total + term
         return total.astype(jnp.bfloat16)
 
@@ -197,11 +197,6 @@
             before = g
         arrived[p, gz] = layer_sum(p, gz)
         block_copy(p, before).start()
-
-    def out_copy(p):
-        v, h = divmod(p, HALVES)
-        at = (v, slice(None), pl.ds(h * half, half))
-        return pltpu.make_async_copy(result.at[at], out_hbm.at[at], osem.at[p])
 
     def finish(p):
         v, h = divmod(p, HALVES)
@@ -217,72 +212,82 @@
                 placed[f] = term if placed[f] is None else placed[f] + term
         for f in range(FRB):
             at = (v, slice(f * width, (f + 1) * width), slice(h * half, (h + 1) * half))
-            result[at] = (front[at].astype(jnp.float32) - placed[f]).astype(jnp.bfloat16)
-        out_copy(p).start()
+            out_ref[at] = (front[at].astype(jnp.float32) - placed[f]).astype(jnp.bfloat16)
+
+    def start_products(p):
+        acc[p] = product(p, row, 1)
+
+    def pair(p, t):
+        acc[p] += product(p, lax.rem(row + t, n_row), 1)
+        acc[p] += product(p, lax.rem(row + n_row - t, n_row), 1)
+
+    def farthest(p):
+        wait_last(p)
+        acc[p] += product(p, lax.rem(row + last + 1, n_row), 1)
 
     parts = 4
+
+    def whole(p):
+        wait_last(p)
+        for q in range(parts):
+            products(p, q, parts)
+
     send_own(0)
+    send_own(1)
     send_l(0)
     for copy in maps:
         copy.wait()
     for v in range(LEVELS):
         rows_of[gz, v] = jnp.full(rows_of.shape[2:], rowmap[0, 0, v], jnp.int32)
-    for p in range(phases):
-        if p == 0:
-            def body(t, _):
-                forward(0, t)
-                return 0
-            lax.fori_loop(1, 3, body, 0)
+
+    starts = (0, 0, last - 2, last + 1)
+    for r in range(1, starts[-1] + last + 1):
+        for p in range(phases):
+            t = r - starts[p]
+            if t == 0:
+                send_own(p)
+            elif 0 < t < last:
+                forward(p, t)
+            elif t == last:
+                forward_last(p)
+        if r == 3:
+            for g in peers:
+                rows_copy(g).start()
+        if r == 4:
             for v in range(1, LEVELS):
                 send_l(v)
-            for g in peers:
-                rows_copy(g).start()
-            lax.fori_loop(3, last, body, 0)
-        elif p < phases - 1:
-            for t in range(1, last):
-                forward(p, t)
-                if t == 1:
-                    wait_last(p - 1)
-                    if p == 1:
-                        wait_l(0)
-                if t <= parts:
-                    products(p - 1, t - 1, parts)
-                if t == parts:
-                    exchange(p - 1)
-                if t == 3 and p >= 2:
-                    finish(p - 2)
-        else:
-            for t in range(1, last):
-                forward(p, t)
-                if t == 1:
-                    wait_last(p - 1)
-                if t <= 2:
-                    products(p - 1, 2 * t - 2, parts)
-                    products(p - 1, 2 * t - 1, parts)
-                if t == 2:
-                    exchange(p - 1)
-                    acc[p % 2] = product(p, row, 1)
-                if t == 3:
-                    finish(p - 2)
-                if t >= 3:
-                    for d in ((1, 2, 3) if t == 3 else (t,)):
-                        acc[p % 2] += product(p, lax.rem(row + d, n_row), 1)
-                        acc[p % 2] += product(p, lax.rem(row + n_row - d, n_row), 1)
-        if p < phases - 1:
-            send_own(p + 1)
-        if p == 0:
+        if r == last + 1:
+            wait_l(0)
+            whole(0)
+            exchange(0)
+        if r == last + 2:
+            whole(1)
+            exchange(1)
+        if r == last + 3:
             fronts.wait()
             wait_rows()
-        forward_last(p)
-        if p == 1:
-            wait_l(1)
+            for v in range(1, LEVELS):
+                wait_l(v)
+            finish(0)
+        if r == last + 4:
+            finish(1)
+        for p in range(2, phases):
+            t = r - starts[p]
+            if r == last + 3:
+                if t >= 0:
+                    start_products(p)
+                for d in range(1, t + 1):
+                    pair(p, d)
+            elif r > last + 3:
+                if 1 <= t <= last:
+                    pair(p, t)
+                elif t == last + 1:
+                    farthest(p)
+                    exchange(p)
     p = phases - 1
+    farthest(p)
+    exchange(p)
     finish(p - 1)
-    acc[p % 2] += product(p, lax.rem(row + last, n_row), 1)
-    acc[p % 2] += product(p, lax.rem(row + n_row - last, n_row), 1)
-    wait_last(p)
-    acc[p % 2] += product(p, lax.rem(row + last + 1, n_row), 1)
-    exchange(p)
     finish(p)
 
     for way in range(2):
@@ -296,8 +301,6 @@
     for q in range(phases):
         at = sums.at[q, pl.ds(0, n_gz - 1)]
         pltpu.make_async_copy(at, at, asend.at[q]).wait()
-    for q in range(phases):
-        out_copy(q).wait()
 
 
 def on_device(lpanel, upanel, rowmap, colmap, blockmask, front_blocks):
@@ -314,15 +317,14 @@
         functools.partial(kernel, n_row, n_gz, n_col),
         out_shape=jax.ShapeDtypeStruct(front_blocks.shape, jnp.bfloat16),
         in_specs=[anywhere] * 6,
-        out_specs=anywhere,
+        out_specs=pl.BlockSpec(memory_space=pltpu.VMEM),
         scratch_shapes=[
             pltpu.VMEM((phases, n_row * depth, CB * half), jnp.bfloat16),
             pltpu.VMEM((LEVELS, n_row, width, depth), jnp.bfloat16),
-            pltpu.VMEM((2, width, CB * half), jnp.float32),
+            pltpu.VMEM((phases, width, CB * half), jnp.float32),
             pltpu.VMEM((phases, n_gz, width, half), jnp.bfloat16),
             pltpu.VMEM((phases, n_gz, width, half), jnp.bfloat16),
             pltpu.VMEM((n_gz, LEVELS, 8, 128), jnp.int32),
-            pltpu.VMEM(front_blocks.shape, jnp.bfloat16),
             pltpu.VMEM(front_blocks.shape, jnp.bfloat16),
             pltpu.SMEM((1, 1, LEVELS), jnp.int32),
             pltpu.SMEM(colmap.shape, jnp.int32),
@@ -338,13 +340,17 @@
             dma((phases, CB)),
             dma((LEVELS, lblocks)),
             dma,
-            dma((phases,)),
             dma((3,)),
         ],
         compiler_params=pltpu.CompilerParams(
-            collective_id=0, has_side_effects=True, vmem_limit_bytes=67043328
+            collective_id=0, has_side_effects=True, vmem_limit_bytes=40 * 1024 * 1024
         ),
-    )(lpanel, upanel, jnp.transpose(rowmap, (1, 2, 0)), colmap, blockmask, front_blocks)
+    )(
+        *(
+            pltpu.with_memory_space_constraint(value, pltpu.HBM)
+            for value in (lpanel, upanel, jnp.transpose(rowmap, (1, 2, 0)), colmap, blockmask, front_blocks)
+        )
+    )
 
 
 def solution(mesh):

time: 125 us -> 114 us (0.912)
  Pallas kernels: 123 us -> 113 us
    pallas_call x1, Pallas kernels: 123 us -> 113 us  [on_device(): pl.pallas_call(functools.partial(kernel, n_row, n_gz, n_col), out_shape=j...]
where the time goes in v2:
time: 114 us
  Pallas kernels  113 us (99%)
    pallas_call x1, Pallas kernels, on_device(): pl.pallas_call(functools.partial(kernel, n_row, n_gz, n_col), out_shape=j...  113 us

profile of v2, /device:TPU:1, one launch (start us, length us, event | category | flops | bytes accessed | tf_op | source)
XLA Modules:
  0.0 113.7 jit_solution(16234114054556053007)
XLA Ops:
  0.0 112.9 %shard_map.64 = bf16[2,512,256]{2,1,0:T(8,128)(2,1)S(1)} custom-call(bf16[2,1,256,512]{3,2,1,0:T(8,128)(2,1)} %l_hbm.1, bf16[2,1,128,1024]{3,2,1,0:T(8,128)(2,1)} %u_hbm.1, s32[1,1,2]{2,1,0:T(1,128)} %bitcast.1, s32[2,1,4]{2,1,0:T(1,128)} %colmap_hbm.1, s32[2,1,1,4]{3,2,1,0:T(1,128)} %mask_hbm.1, bf16[2,512,256]{2,1,0:T(8,128)(2,1)} %front_hbm.1), custom_call_target="tpu_custom_call" | custom-call | tf_op jit(solution)/shard_map/pallas_call | solution.py:316
  112.9 0.8 copy.8

commit v3 on v2

--- a/solution.py
+++ b/solution.py
@@ -12,7 +12,8 @@
 FRB = 2
 LEVELS = 2
 HALVES = 2
-SUBS = 4
+SUBS = (2, 2, 4, 4)
+SLOTS = 3
 
 
 def kernel(
@@ -30,7 +31,6 @@
     half = width // HALVES
     lblocks = l_hbm.shape[3] // depth
     last = n_row // 2 - 1
-    piece = depth // SUBS
     ring = [lax.rem(row + 1, n_row), lax.rem(row + n_row - 1, n_row)]
 
     def others(me, n):
@@ -46,17 +46,25 @@
             if (d, k) != (0, 0):
                 peers.append(lax.rem(chip + d, chips) * cores + lax.rem(core + k, cores))
 
+    barrier = pltpu.get_barrier_semaphore()
+    for r in ring:
+        pl.semaphore_signal(barrier, inc=1, device_id={"row": r}, device_id_type=MESH)
+    for c in others(col, n_col):
+        pl.semaphore_signal(barrier, inc=1, device_id={"col": c}, device_id_type=MESH)
+    for g in peers:
+        pl.semaphore_signal(barrier, inc=1, device_id={"gz": g}, device_id_type=MESH)
+
     def own_u(p, j):
         v, h = divmod(p, HALVES)
         return pltpu.make_async_copy(
             u_hbm.at[v, 0, :, pl.ds(j * width + h * half, half)],
             u_all.at[p, pl.ds(row * depth, depth), pl.ds(j * half, half)],
-            usem.at[p, j],
+            usem.at[p],
         )
 
     def own_l(v, i):
         return pltpu.make_async_copy(
-            l_hbm.at[v, 0, :, pl.ds(i * depth, depth)], l_all.at[v, col * lblocks + i], lsem.at[v, i]
+            l_hbm.at[v, 0, :, pl.ds(i * depth, depth)], l_all.at[v, col * lblocks + i], lsem.at[v]
         )
 
     fronts = pltpu.make_async_copy(front_hbm, front, fsem)
@@ -79,85 +87,74 @@
     for copy in maps:
         copy.start()
 
-    barrier = pltpu.get_barrier_semaphore()
-    for r in ring:
-        pl.semaphore_signal(barrier, inc=1, device_id={"row": r}, device_id_type=MESH)
-    for c in others(col, n_col):
-        pl.semaphore_signal(barrier, inc=1, device_id={"col": c}, device_id_type=MESH)
-    for g in peers:
-        pl.semaphore_signal(barrier, inc=1, device_id={"gz": g}, device_id_type=MESH)
     pl.semaphore_wait(barrier, 2 + (n_col - 1) + (n_gz - 1))
+
+    def landed(way, p, t, s):
+        return zrecv.at[way, SLOTS * sum(SUBS[:p]) + (t % SLOTS) * SUBS[p] + s]
 
     def hop(way, p, t, s):
         shard = lax.rem(row + n_row - t, n_row) if way == 0 else lax.rem(row + t, n_row)
+        piece = depth // SUBS[p]
         at = u_all.at[p, pl.ds(pl.multiple_of(shard * depth + s * piece, piece), piece)]
         return pltpu.make_async_remote_copy(
-            src_ref=at, dst_ref=at, send_sem=zsend.at[way, p], recv_sem=zrecv.at[way, p, t, s],
+            src_ref=at, dst_ref=at, send_sem=zsend, recv_sem=landed(way, p, t, s),
             device_id={"row": ring[way]}, device_id_type=MESH,
         )
 
     def arrival(way, p, t, s):
-        at = u_all.at[p, pl.ds(0, piece)]
-        return pltpu.make_async_copy(at, at, zrecv.at[way, p, t, s])
-
-    longer = (range(SUBS // 2), range(SUBS // 2, SUBS))
+        at = u_all.at[p, pl.ds(0, depth // SUBS[p])]
+        return pltpu.make_async_copy(at, at, landed(way, p, t, s))
+
+    def longer(way, p):
+        return range(SUBS[p] // 2) if way == 0 else range(SUBS[p] // 2, SUBS[p])
+
+    def each(p):
+        return [(way, (s + way * SUBS[p] // 2) % SUBS[p]) for s in range(SUBS[p]) for way in range(2)]
 
     def send_own(p):
-        for j in range(CB):
-            own_u(p, j).wait()
-        for s in range(SUBS):
-            for way in range(2):
-                hop(way, p, 0, (s + way * SUBS // 2) % SUBS).start()
+        at = u_all.at[p, pl.ds(0, depth)]
+        pltpu.make_async_copy(at, at, usem.at[p]).wait()
+        for way, k in each(p):
+            hop(way, p, 0, k).start()
 
     def forward(p, t):
-        for s in range(SUBS):
-            for way in range(2):
-                which = (s + way * SUBS // 2) % SUBS
-                arrival(way, p, t - 1, which).wait()
-                hop(way, p, t, which).start()
-
-    def forward_last(p):
-        for s in range(SUBS):
-            for way in range(2):
-                which = (s + way * SUBS // 2) % SUBS
-                arrival(way, p, last - 1, which).wait()
-                if which in longer[way]:
-                    hop(way, p, last, which).start()
+        for way, k in each(p):
+            arrival(way, p, t - 1, k).wait()
+            if t < last or k in longer(way, p):
+                hop(way, p, t, k).start()
 
     def wait_last(p):
         for way in range(2):
-            for s in longer[way]:
-                arrival(way, p, last, s).wait()
+            for k in longer(way, p):
+                arrival(way, p, last, k).wait()
 
     def l_copy(v, c):
         at = l_all.at[v, pl.ds(col * lblocks, lblocks)]
         return pltpu.make_async_remote_copy(
-            src_ref=at, dst_ref=at, send_sem=lsend, recv_sem=lrecv.at[v, col],
+            src_ref=at, dst_ref=at, send_sem=lsend, recv_sem=lrecv.at[v],
             device_id={"col": c}, device_id_type=MESH,
         )
 
     def send_l(v):
-        for i in range(lblocks):
-            own_l(v, i).wait()
+        at = l_all.at[v, pl.ds(0, lblocks)]
+        pltpu.make_async_copy(at, at, lsem.at[v]).wait()
         for c in others(col, n_col):
             l_copy(v, c).start()
 
     def wait_l(v):
-        at = l_all.at[v, pl.ds(0, lblocks)]
-        for c in others(col, n_col):
-            pltpu.make_async_copy(at, at, lrecv.at[v, c]).wait()
+        at = l_all.at[v, pl.ds(0, (n_col - 1) * lblocks)]
+        pltpu.make_async_copy(at, at, lrecv.at[v]).wait()
 
     def rows_copy(g):
         at = rows_of.at[gz]
         return pltpu.make_async_remote_copy(
-            src_ref=at, dst_ref=at, send_sem=rsend, recv_sem=rrecv.at[gz],
+            src_ref=at, dst_ref=at, send_sem=rsend, recv_sem=rrecv,
             device_id={"gz": g}, device_id_type=MESH,
         )
 
     def wait_rows():
-        at = rows_of.at[0]
-        for g in peers:
-            pltpu.make_async_copy(at, at, rrecv.at[g]).wait()
+        at = rows_of.at[pl.ds(0, n_gz - 1)]
+        pltpu.make_async_copy(at, at, rrecv).wait()
 
     def product(p, first, count):
         v = p // HALVES
@@ -175,7 +172,7 @@
 
     def block_copy(p, g):
         return pltpu.make_async_remote_copy(
-            src_ref=sums.at[p, g], dst_ref=arrived.at[p, gz], send_sem=asend.at[p], recv_sem=arecv.at[p, gz],
+            src_ref=sums.at[p, g], dst_ref=arrived.at[p, gz], send_sem=asend, recv_sem=arecv.at[p],
             device_id={"gz": g}, device_id_type=MESH,
         )
 
@@ -200,9 +197,8 @@
 
     def finish(p):
         v, h = divmod(p, HALVES)
-        block = arrived.at[p, 0]
-        for g in peers:
-            pltpu.make_async_copy(block, block, arecv.at[p, g]).wait()
+        block = arrived.at[p, pl.ds(0, n_gz - 1)]
+        pltpu.make_async_copy(block, block, arecv.at[p]).wait()
         placed = [None] * FRB
         for g in range(n_gz):
             value = arrived[p, g].astype(jnp.float32)
@@ -246,10 +242,8 @@
             t = r - starts[p]
             if t == 0:
                 send_own(p)
-            elif 0 < t < last:
+            elif 0 < t <= last:
                 forward(p, t)
-            elif t == last:
-                forward_last(p)
         if r == 3:
             for g in peers:
                 rows_copy(g).start()
@@ -290,17 +284,15 @@
     finish(p - 1)
     finish(p)
 
-    for way in range(2):
-        for q in range(phases):
-            at = u_all.at[q, pl.ds(0, depth * last + depth // 2)]
-            pltpu.make_async_copy(at, at, zsend.at[way, q]).wait()
-    at = l_all.at[pl.ds(0, LEVELS), pl.ds(0, (n_col - 1) * lblocks)]
+    hops = 2 * last + 1
+    at = u_all.at[:, pl.ds(0, depth * hops)]
+    pltpu.make_async_copy(at, at, zsend).wait()
+    at = l_all.at[:, pl.ds(0, (n_col - 1) * lblocks)]
     pltpu.make_async_copy(at, at, lsend).wait()
     at = rows_of.at[pl.ds(0, n_gz - 1)]
     pltpu.make_async_copy(at, at, rsend).wait()
-    for q in range(phases):
-        at = sums.at[q, pl.ds(0, n_gz - 1)]
-        pltpu.make_async_copy(at, at, asend.at[q]).wait()
+    at = sums.at[:, pl.ds(0, n_gz - 1)]
+    pltpu.make_async_copy(at, at, asend).wait()
 
 
 def on_device(lpanel, upanel, rowmap, colmap, blockmask, front_blocks):
@@ -310,7 +302,6 @@
     half = width // HALVES
     phases = LEVELS * HALVES
     lblocks = lpanel.shape[3] // depth
-    hops = n_row // 2
     anywhere = pl.BlockSpec(memory_space=pltpu.HBM)
     dma = pltpu.SemaphoreType.DMA
     return pl.pallas_call(
@@ -329,16 +320,16 @@
             pltpu.SMEM((1, 1, LEVELS), jnp.int32),
             pltpu.SMEM(colmap.shape, jnp.int32),
             pltpu.SMEM(blockmask.shape, jnp.int32),
-            dma((2, phases)),
-            dma((2, phases, hops, SUBS)),
-            dma,
-            dma((LEVELS, n_col)),
+            dma,
+            dma((2, SLOTS * sum(SUBS))),
+            dma,
+            dma((LEVELS,)),
+            dma,
             dma((phases,)),
-            dma((phases, n_gz)),
-            dma,
-            dma((n_gz,)),
-            dma((phases, CB)),
-            dma((LEVELS, lblocks)),
+            dma,
+            dma,
+            dma((phases,)),
+            dma((LEVELS,)),
             dma,
             dma((3,)),
         ],

time: 114 us -> 111 us (0.974)
  Pallas kernels: 113 us -> 111 us
    pallas_call x1, Pallas kernels: 113 us -> 111 us  [on_device(): pl.pallas_call(functools.partial(kernel, n_row, n_gz, n_col), out_shape=j...]
where the time goes in v3:
time: 111 us
  Pallas kernels  111 us (100%)
    pallas_call x1, Pallas kernels, on_device(): pl.pallas_call(functools.partial(kernel, n_row, n_gz, n_col), out_shape=j...  111 us

profile of v3, /device:TPU:1, one launch (start us, length us, event | category | flops | bytes accessed | tf_op | source)
XLA Modules:
  0.0 111.3 jit_solution(8724828398541856988)
XLA Ops:
  0.0 110.5 %shard_map.64 = bf16[2,512,256]{2,1,0:T(8,128)(2,1)S(1)} custom-call(bf16[2,1,256,512]{3,2,1,0:T(8,128)(2,1)} %l_hbm.1, bf16[2,1,128,1024]{3,2,1,0:T(8,128)(2,1)} %u_hbm.1, s32[1,1,2]{2,1,0:T(1,128)} %bitcast.1, s32[2,1,4]{2,1,0:T(1,128)} %colmap_hbm.1, s32[2,1,1,4]{3,2,1,0:T(1,128)} %mask_hbm.1, bf16[2,512,256]{2,1,0:T(8,128)(2,1)} %front_hbm.1), custom_call_target="tpu_custom_call" | custom-call | tf_op jit(solution)/shard_map/pallas_call | solution.py:307
  110.6 0.8 copy.8

commit v4 on v3

--- a/solution.py
+++ b/solution.py
@@ -12,8 +12,9 @@
 FRB = 2
 LEVELS = 2
 HALVES = 2
-SUBS = (2, 2, 4, 4)
+SUBS = (1, 1, 4, 4)
 SLOTS = 3
+EARLY = 1
 
 
 def kernel(
@@ -22,7 +23,7 @@
     out_ref,
     u_all, l_all, acc, sums, arrived, rows_of, front,
     rowmap, colmap, mask,
-    zsend, zrecv, lsend, lrecv, asend, arecv, rsend, rrecv, usem, lsem, fsem, isem,
+    zsend, zrecv, lsend, lrecv, asend, arecv, rsend, rrecv, usem, lsem, fsem, isem, vouch,
 ):
     row, gz, col = lax.axis_index("row"), lax.axis_index("gz"), lax.axis_index("col")
     phases = LEVELS * HALVES
@@ -45,14 +46,23 @@
         for k in range(cores):
             if (d, k) != (0, 0):
                 peers.append(lax.rem(chip + d, chips) * cores + lax.rem(core + k, cores))
+    early = [jnp.where(gz == EARLY, peers[0], EARLY)]
+    early += [jnp.where(g == EARLY, peers[0], g) for g in peers[1:]]
 
     barrier = pltpu.get_barrier_semaphore()
+    near_gz = [
+        lax.rem(chip + d, chips) * cores + lax.rem(core + k, cores)
+        for d in (0, 1, chips - 1)
+        for k in range(cores)
+        if (d, k) != (0, 0)
+    ]
+    near_col = [lax.rem(col + 1, n_col), lax.rem(col + n_col - 1, n_col)]
     for r in ring:
         pl.semaphore_signal(barrier, inc=1, device_id={"row": r}, device_id_type=MESH)
-    for c in others(col, n_col):
+    for g in near_gz:
+        pl.semaphore_signal(barrier, inc=1, device_id={"gz": g}, device_id_type=MESH)
+    for c in near_col:
         pl.semaphore_signal(barrier, inc=1, device_id={"col": c}, device_id_type=MESH)
-    for g in peers:
-        pl.semaphore_signal(barrier, inc=1, device_id={"gz": g}, device_id_type=MESH)
 
     def own_u(p, j):
         v, h = divmod(p, HALVES)
@@ -73,21 +83,11 @@
         pltpu.make_async_copy(colmap_hbm, colmap, isem.at[1]),
         pltpu.make_async_copy(mask_hbm, mask, isem.at[2]),
     ]
-    for j in range(CB):
-        own_u(0, j).start()
-    for i in range(lblocks):
-        own_l(0, i).start()
-    for p in range(1, phases):
+    for p in range(2):
         for j in range(CB):
             own_u(p, j).start()
-    for v in range(1, LEVELS):
-        for i in range(lblocks):
-            own_l(v, i).start()
-    fronts.start()
-    for copy in maps:
-        copy.start()
-
-    pl.semaphore_wait(barrier, 2 + (n_col - 1) + (n_gz - 1))
+
+    pl.semaphore_wait(barrier, len(ring) + len(near_gz) + len(near_col))
 
     def landed(way, p, t, s):
         return zrecv.at[way, SLOTS * sum(SUBS[:p]) + (t % SLOTS) * SUBS[p] + s]
@@ -106,6 +106,8 @@
         return pltpu.make_async_copy(at, at, landed(way, p, t, s))
 
     def longer(way, p):
+        if SUBS[p] == 1:
+            return range(1) if way == p % 2 else range(0)
         return range(SUBS[p] // 2) if way == 0 else range(SUBS[p] // 2, SUBS[p])
 
     def each(p):
@@ -156,19 +158,13 @@
         at = rows_of.at[pl.ds(0, n_gz - 1)]
         pltpu.make_async_copy(at, at, rrecv).wait()
 
-    def product(p, first, count):
+    def product(p, shards):
         v = p // HALVES
-        left = jnp.concatenate([l_all[v, first + i] for i in range(count)], axis=1) if count > 1 else l_all[v, first]
-        right = u_all[p, pl.ds(pl.multiple_of(first * depth, depth), count * depth), :]
-        return jnp.dot(left, right, preferred_element_type=jnp.float32)
-
-    def products(p, q, parts):
-        size = n_row // parts
-        value = product(p, q * size, size)
-        if q == 0:
-            acc[p] = value
-        else:
-            acc[p] += value
+        left = [l_all[v, k] for k in shards]
+        right = [u_all[p, pl.ds(pl.multiple_of(k * depth, depth), depth), :] for k in shards]
+        if len(shards) > 1:
+            left, right = [jnp.concatenate(left, axis=1)], [jnp.concatenate(right, axis=0)]
+        return jnp.dot(left[0], right[0], preferred_element_type=jnp.float32)
 
     def block_copy(p, g):
         return pltpu.make_async_remote_copy(
@@ -187,7 +183,7 @@
 
     def exchange(p):
         before = None
-        for g in peers:
+        for g in early:
             sums[p, g] = layer_sum(p, g)
             if before is not None:
                 block_copy(p, before).start()
@@ -210,74 +206,75 @@
             at = (v, slice(f * width, (f + 1) * width), slice(h * half, (h + 1) * half))
             out_ref[at] = (front[at].astype(jnp.float32) - placed[f]).astype(jnp.bfloat16)
 
-    def start_products(p):
-        acc[p] = product(p, row, 1)
-
-    def pair(p, t):
-        acc[p] += product(p, lax.rem(row + t, n_row), 1)
-        acc[p] += product(p, lax.rem(row + n_row - t, n_row), 1)
+    def near(p, t):
+        if t == 0:
+            acc[p] = product(p, [row])
+        else:
+            acc[p] += product(p, [lax.rem(row + t, n_row), lax.rem(row + n_row - t, n_row)])
 
     def farthest(p):
         wait_last(p)
-        acc[p] += product(p, lax.rem(row + last + 1, n_row), 1)
-
-    parts = 4
-
-    def whole(p):
-        wait_last(p)
-        for q in range(parts):
-            products(p, q, parts)
+        acc[p] += product(p, [lax.rem(row + last + 1, n_row)])
 
     send_own(0)
     send_own(1)
-    send_l(0)
+    for v in range(LEVELS):
+        for i in range(lblocks):
+            own_l(v, i).start()
+    for copy in maps:
+        copy.start()
+    for p in range(2, phases):
+        for j in range(CB):
+            own_u(p, j).start()
+    fronts.start()
+    pl.semaphore_signal(
+        vouch.at[0], inc=1, device_id={"gz": lax.rem(chip + 1, chips) * cores + core}, device_id_type=MESH
+    )
+    pl.semaphore_signal(vouch.at[1], inc=1, device_id={"col": near_col[0]}, device_id_type=MESH)
+    pl.semaphore_wait(vouch.at[1], 1)
+    for v in range(LEVELS):
+        send_l(v)
     for copy in maps:
         copy.wait()
     for v in range(LEVELS):
         rows_of[gz, v] = jnp.full(rows_of.shape[2:], rowmap[0, 0, v], jnp.int32)
 
-    starts = (0, 0, last - 2, last + 1)
+    starts = (0, 0, last - 2, last)
+    begin = (3, 4, 0, 0)
     for r in range(1, starts[-1] + last + 1):
+        if r == 2:
+            pl.semaphore_wait(vouch.at[0], 1)
+            for g in peers:
+                rows_copy(g).start()
+        if r == begin[0]:
+            wait_l(0)
+        if r == starts[2]:
+            for v in range(1, LEVELS):
+                wait_l(v)
+        if r == starts[2] + last + 1:
+            farthest(2)
+            exchange(2)
         for p in range(phases):
             t = r - starts[p]
             if t == 0:
                 send_own(p)
             elif 0 < t <= last:
                 forward(p, t)
-        if r == 3:
-            for g in peers:
-                rows_copy(g).start()
-        if r == 4:
-            for v in range(1, LEVELS):
-                send_l(v)
+            if begin[p] <= t <= last:
+                for d in range(0 if t == begin[p] else t, t + 1):
+                    near(p, d)
         if r == last + 1:
-            wait_l(0)
-            whole(0)
+            farthest(0)
             exchange(0)
         if r == last + 2:
-            whole(1)
+            farthest(1)
             exchange(1)
         if r == last + 3:
             fronts.wait()
             wait_rows()
-            for v in range(1, LEVELS):
-                wait_l(v)
             finish(0)
         if r == last + 4:
             finish(1)
-        for p in range(2, phases):
-            t = r - starts[p]
-            if r == last + 3:
-                if t >= 0:
-                    start_products(p)
-                for d in range(1, t + 1):
-                    pair(p, d)
-            elif r > last + 3:
-                if 1 <= t <= last:
-                    pair(p, t)
-                elif t == last + 1:
-                    farthest(p)
-                    exchange(p)
     p = phases - 1
     farthest(p)
     exchange(p)
@@ -332,6 +329,7 @@
             dma((LEVELS,)),
             dma,
             dma((3,)),
+            pltpu.SemaphoreType.REGULAR((2,)),
         ],
         compiler_params=pltpu.CompilerParams(
             collective_id=0, has_side_effects=True, vmem_limit_bytes=40 * 1024 * 1024

time: 111 us -> 109 us (0.982)
  Pallas kernels: 111 us -> 108 us
    pallas_call x1, Pallas kernels: 111 us -> 108 us  [on_device(): pl.pallas_call(functools.partial(kernel, n_row, n_gz, n_col), out_shape=j...]
where the time goes in v4:
time: 109 us
  Pallas kernels  108 us (99%)
    pallas_call x1, Pallas kernels, on_device(): pl.pallas_call(functools.partial(kernel, n_row, n_gz, n_col), out_shape=j...  108 us

profile of v4, /device:TPU:1, one launch (start us, length us, event | category | flops | bytes accessed | tf_op | source)
XLA Modules:
  0.0 109.3 jit_solution(11667076423592275261)
XLA Ops:
  0.0 108.5 %shard_map.64 = bf16[2,512,256]{2,1,0:T(8,128)(2,1)S(1)} custom-call(bf16[2,1,256,512]{3,2,1,0:T(8,128)(2,1)} %l_hbm.1, bf16[2,1,128,1024]{3,2,1,0:T(8,128)(2,1)} %u_hbm.1, s32[1,1,2]{2,1,0:T(1,128)} %bitcast.1, s32[2,1,4]{2,1,0:T(1,128)} %colmap_hbm.1, s32[2,1,1,4]{3,2,1,0:T(1,128)} %mask_hbm.1, bf16[2,512,256]{2,1,0:T(8,128)(2,1)} %front_hbm.1), custom_call_target="tpu_custom_call" | custom-call | tf_op jit(solution)/shard_map/pallas_call | solution.py:304
  108.5 0.8 copy.8

commit v5 on v4

--- a/solution.py
+++ b/solution.py
@@ -40,7 +40,7 @@
     cores = 2
     chips = n_gz // cores
     chip, core = lax.div(gz, cores), lax.rem(gz, cores)
-    order = sorted(range(1, chips), key=lambda d: -min(d, chips - d)) + [0]
+    order = sorted(range(1, chips), key=lambda d: min(d, chips - d)) + [0]
     peers = []
     for d in order:
         for k in range(cores):

time: 109 us -> 109 us (level)
  no operation moved by 1% of the time
where the time goes in v5:
time: 109 us
  Pallas kernels  108 us (99%)
    pallas_call x1, Pallas kernels, on_device(): pl.pallas_call(functools.partial(kernel, n_row, n_gz, n_col), out_shape=j...  108 us

profile of v5, /device:TPU:1, one launch (start us, length us, event | category | flops | bytes accessed | tf_op | source)
XLA Modules:
  0.0 108.6 jit_solution(9567453584439245117)
XLA Ops:
  0.0 107.8 %shard_map.64 = bf16[2,512,256]{2,1,0:T(8,128)(2,1)S(1)} custom-call(bf16[2,1,256,512]{3,2,1,0:T(8,128)(2,1)} %l_hbm.1, bf16[2,1,128,1024]{3,2,1,0:T(8,128)(2,1)} %u_hbm.1, s32[1,1,2]{2,1,0:T(1,128)} %bitcast.1, s32[2,1,4]{2,1,0:T(1,128)} %colmap_hbm.1, s32[2,1,1,4]{3,2,1,0:T(1,128)} %mask_hbm.1, bf16[2,512,256]{2,1,0:T(8,128)(2,1)} %front_hbm.1), custom_call_target="tpu_custom_call" | custom-call | tf_op jit(solution)/shard_map/pallas_call | solution.py:304
  107.8 0.8 copy.8

commit v6 on v5

--- a/solution.py
+++ b/solution.py
@@ -168,7 +168,7 @@
 
     def block_copy(p, g):
         return pltpu.make_async_remote_copy(
-            src_ref=sums.at[p, g], dst_ref=arrived.at[p, gz], send_sem=asend, recv_sem=arecv.at[p],
+            src_ref=sums.at[p, g], dst_ref=arrived.at[p, gz], send_sem=asend, recv_sem=arecv.at[p + gz if p == phases - 1 else p],
             device_id={"gz": g}, device_id_type=MESH,
         )
 
@@ -193,10 +193,15 @@
 
     def finish(p):
         v, h = divmod(p, HALVES)
-        block = arrived.at[p, pl.ds(0, n_gz - 1)]
-        pltpu.make_async_copy(block, block, arecv.at[p]).wait()
+        final = p == phases - 1
+        if not final:
+            block = arrived.at[p, pl.ds(0, n_gz - 1)]
+            pltpu.make_async_copy(block, block, arecv.at[p]).wait()
         placed = [None] * FRB
-        for g in range(n_gz):
+        for g in [gz, peers[-1], *peers[:-1]] if final else range(n_gz):
+            if final and g is not gz:
+                block = arrived.at[p, 0]
+                pltpu.make_async_copy(block, block, arecv.at[p + g]).wait()
             value = arrived[p, g].astype(jnp.float32)
             target = rows_of[g, v][:1]
             for f in range(FRB):
@@ -322,7 +327,7 @@
             dma,
             dma((LEVELS,)),
             dma,
-            dma((phases,)),
+            dma((phases - 1 + n_gz,)),
             dma,
             dma,
             dma((phases,)),

time: 109 us -> 109 us (level)
  no operation moved by 1% of the time
where the time goes in v6:
time: 109 us
  Pallas kernels  108 us (99%)
    pallas_call x1, Pallas kernels, on_device(): pl.pallas_call(functools.partial(kernel, n_row, n_gz, n_col), out_shape=j...  108 us

profile of v6, /device:TPU:1, one launch (start us, length us, event | category | flops | bytes accessed | tf_op | source)
XLA Modules:
  0.0 108.5 jit_solution(6928166310596469942)
XLA Ops:
  0.0 107.7 %shard_map.64 = bf16[2,512,256]{2,1,0:T(8,128)(2,1)S(1)} custom-call(bf16[2,1,256,512]{3,2,1,0:T(8,128)(2,1)} %l_hbm.1, bf16[2,1,128,1024]{3,2,1,0:T(8,128)(2,1)} %u_hbm.1, s32[1,1,2]{2,1,0:T(1,128)} %bitcast.1, s32[2,1,4]{2,1,0:T(1,128)} %colmap_hbm.1, s32[2,1,1,4]{3,2,1,0:T(1,128)} %mask_hbm.1, bf16[2,512,256]{2,1,0:T(8,128)(2,1)} %front_hbm.1), custom_call_target="tpu_custom_call" | custom-call | tf_op jit(solution)/shard_map/pallas_call | solution.py:309
  107.7 0.8 copy.8
